TPU v7x, 32 devices: a whole 2x2x4 slice. The times are simulated.
32 devices in a mesh: gx: 8 (over z, core), gy: 4 (over y, x).
Axes of the slice: x: 2, y: 2, z: 4, core: 2. Of those that a mesh axis runs over, the one named last changes fastest.
Arguments:
- density: float32 [512, 512, 512], P('gx', 'gy'), may hold values from -6 to 6
- radius_cells: int32 [2], replicated, may hold values from 1 to 32
Outputs:
- filtered: float32 [2, 512, 512, 512], P(None, 'gx', 'gy')
All inputs are finite; a program needn't handle non-finite values.
Results may differ from a plain program's by a relative error of at most 0.0001.
Values sent between devices are 32-bit elements; how exact they have to be, the bound alone decides.
A program may use at most 192 MiB of HBM per device.

v0:
```python
import math

import jax
import jax.numpy as jnp
import numpy as np
from jax import lax
from jax.sharding import PartitionSpec as P

PREC = lax.Precision.HIGH


def window(k_squared, scale_squared):
    u_squared = k_squared * scale_squared
    u_value = jnp.sqrt(u_squared)
    is_small = u_value < 0.2
    safe = jnp.where(is_small, 1.0, u_value)
    turns = jnp.floor(safe * (1.0 / math.pi) + 0.5)
    rest = safe - turns * 3.140625
    rest = rest - turns * 9.67502593994140625e-4
    rest = rest - turns * 1.509957990978376432e-7
    s2 = rest * rest
    sin_v = rest * (1.0 + s2 * (-1.6666666666e-1 + s2 * (8.3333333e-3 + s2 * (
        -1.98412698e-4 + s2 * (2.75573192e-6 + s2 * -2.50521084e-8)))))
    cos_v = 1.0 + s2 * (-0.5 + s2 * (4.16666666e-2 + s2 * (-1.38888889e-3 + s2 * (
        2.48015873e-5 + s2 * (-2.75573192e-7 + s2 * 2.08767570e-9)))))
    half = turns * 0.5
    sign = jnp.where(half == jnp.floor(half), 3.0, -3.0)
    closed = sign * (sin_v - safe * cos_v) / (safe * safe * safe)
    series = 1.0 - u_squared / 10.0 + u_squared * u_squared / 280.0
    return jnp.where(is_small, series, closed)


def times_i(values, half):
    return jnp.concatenate([-values[..., half:], values[..., :half]], -1)


def doubled(values, half):
    return jnp.concatenate([values, times_i(values, half)], 0)


def squares(values, length):
    signed = jnp.where(values > length // 2, values - length, values).astype(jnp.float32)
    return signed * signed


def dot(spec, left, right):
    return jnp.einsum(spec, left, right, precision=PREC, preferred_element_type=jnp.float32)


def trig(rows, cols, length):
    angles = 2.0 * math.pi / length * (np.outer(rows, cols) % length)
    return np.cos(angles), np.sin(angles)


def y_order(length, parts):
    half = length // parts // 2
    base = np.arange(length // 2).reshape(parts, half)
    mirror = (length - base) % length
    mirror[0, 0] = length // 2
    return np.concatenate([base, mirror], 1).reshape(-1)


def per_device(density, radius_cells):
    rows_x, rows_y, length = density.shape
    count_gx = lax.axis_size("gx")
    count_gy = lax.axis_size("gy")
    mid = length // 2
    half = mid // count_gy
    lanes = 2 * half
    cols_y = length // count_gx
    f32 = jnp.float32
    cells = np.arange(length)
    order = y_order(length, count_gx)

    cos_z, sin_z = trig(cells, np.arange(mid), length)
    fwd_im = -sin_z
    fwd_im[:, 0] = np.where(cells % 2 == 0, 1.0, -1.0)
    fwd_z = np.stack([cos_z, fwd_im], 1).reshape(length, 2, count_gy, half)
    fwd_z = jnp.asarray(fwd_z.transpose(2, 0, 1, 3).reshape(count_gy, length, lanes), f32)
    gain = np.full((mid,), 2.0 / float(length) ** 3)
    gain[0] = 1.0 / float(length) ** 3
    inv_re = cos_z * gain
    inv_im = -sin_z * gain
    inv_im[:, 0] = np.where(cells % 2 == 0, 1.0, -1.0) * gain[0]
    inv_z = np.stack([inv_re, inv_im], 1).reshape(length, 2, count_gy, half)
    inv_z = jnp.asarray(inv_z.transpose(2, 1, 3, 0).reshape(length, length), f32)
    cos_y, sin_y = trig(order, cells, length)
    fwd_y = jnp.asarray(np.concatenate([cos_y, sin_y], 1), f32)
    fwd_y = fwd_y * jnp.where(jnp.arange(2 * length) < length, 1.0, -1.0)
    inv_y = jnp.asarray(np.concatenate([cos_y.T, sin_y.T], 1), f32)
    cos_x, sin_x = trig(cells, cells, length)
    inv_x = jnp.asarray(np.concatenate([cos_x, sin_x], 1), f32)
    fwd_x = inv_x * jnp.where(jnp.arange(2 * length) < length, 1.0, -1.0)

    values = dot("xyz,bzl->byxl", density, fwd_z)
    values = lax.all_to_all(values, "gy", split_axis=0, concat_axis=0, tiled=True)
    values = values.reshape(length, rows_x, lanes)
    values = dot("qy,yxl->qxl", fwd_y, doubled(values, half))
    values = values.reshape(count_gx, cols_y, rows_x, lanes).transpose(0, 2, 1, 3)
    values = lax.all_to_all(values, "gx", split_axis=0, concat_axis=0, tiled=True)
    values = values.reshape(length, cols_y, lanes)
    values = dot("kx,xql->kql", fwd_x, doubled(values, half))

    part_x = lax.axis_index("gx")
    part_y = lax.axis_index("gy")
    kx_sq = squares(jnp.arange(length, dtype=jnp.int32), length)
    local = jnp.arange(cols_y, dtype=jnp.int32)
    base = part_x * (cols_y // 2) + local % (cols_y // 2)
    ky = jnp.where(local < cols_y // 2, base, (length - base) % length)
    ky = jnp.where((part_x == 0) & (local == cols_y // 2), mid, ky)
    ky_sq = squares(ky, length)
    lane = jnp.arange(lanes, dtype=jnp.int32)
    kz_sq = squares(part_y * half + lane % half, length)
    plane_sq = kx_sq[:, None] + ky_sq[None, :]
    cube_sq = plane_sq[:, :, None] + kz_sq[None, None, :]

    own_re = values[:, :, 0]
    own_im = values[:, :, half]

    def mirror(plane):
        plane = jnp.roll(jnp.flip(plane, 0), 1, 0)
        swapped = jnp.roll(plane, cols_y // 2, 1)
        itself = (part_x == 0) & (local % (cols_y // 2) == 0)
        return jnp.where(itself[None, :], plane, swapped)

    far_re, far_im = mirror(own_re), mirror(own_im)
    first = part_y == 0
    outs = []
    for index in range(radius_cells.shape[0]):
        scale = 2.0 * math.pi / length * radius_cells[index].astype(f32)
        scale = scale * scale
        weight = window(cube_sq, scale)
        low = window(plane_sq, scale)
        high = window(plane_sq + float(mid) ** 2, scale)
        mean, diff = 0.5 * (low + high), 0.5 * (low - high)
        fix_re = own_re * mean + far_re * diff
        fix_im = own_im * mean - far_im * diff
        field = values * weight
        field = jnp.where(first & (lane == 0), fix_re[:, :, None], field)
        field = jnp.where(first & (lane == half), fix_im[:, :, None], field)
        field = dot("xk,kql->xql", inv_x, doubled(field, half))
        field = field.reshape(count_gx, rows_x, cols_y, lanes)
        outs.append(lax.all_to_all(field, "gx", split_axis=0, concat_axis=0, tiled=True))
    results = []
    for field in outs:
        field = field.transpose(0, 2, 1, 3).reshape(length, rows_x, lanes)
        field = dot("yq,qxl->yxl", inv_y, doubled(field, half))
        field = field.reshape(count_gy, rows_y, rows_x, lanes)
        field = lax.all_to_all(field, "gy", split_axis=0, concat_axis=0, tiled=True)
        field = dot("gyxl,glz->xyz", field, inv_z.reshape(count_gy, lanes, length))
        results.append(field)
    return jnp.stack(results)


def solution(mesh):
    return jax.shard_map(
        per_device,
        mesh=mesh,
        in_specs=(P("gx", "gy", None), P()),
        out_specs=P(None, "gx", "gy", None),
        check_vma=False,
    )
```

profile of v0, /device:TPU:11, one launch (start us, length us, event | category | flops | bytes accessed | tf_op | source)
XLA Modules:
  0.0 2029.1 jit_solution(5555310782021072428)
XLA Ops:
  0.0 18.9 fusion.84
  26.1 181.4 %all-to-all-done = f32[4,128,64,128]{1,3,2,0:T(8,128)} async-done(((f32[4,128,64,128]{1,3,2,0:T(8,128)}), f32[4,128,64,128]{1,3,2,0:T(8,128)}, u32[]{:S(2)}, u32[]{:S(2)}) %all-to-all-start) | async-done | bytes 16777248 | tf_op jit(solution)/shard_map/all_to_all | solution.py:96
  207.5 17.5 copy.70
  225.0 23.7 %slice_negate_fusion.2 = (f32[512,64,64]{2,0,1:T(8,128)}, f32[512,64,64]{2,0,1:T(8,128)}) fusion(f32[512,64,128]{2,0,1:T(8,128)} %bitcast.94), kind=kLoop, calls=%fused_computation.80 | loop fusion | flops 2097152 | bytes 33554432 | tf_op jit(solution)/shard_map/neg | solution.py:34
  248.7 36.8 %fusion = f32[512,64,128]{2,0,1:T(8,128)} fusion(f32[512,64,64]{2,0,1:T(8,128)} %get-tuple-element.24, f32[512,64,64]{2,0,1:T(8,128)} %get-tuple-element.23, f32[512,64,128]{2,0,1:T(8,128)} %bitcast.95, f32[512,1024]{1,0:T(8,128)S(1)} %copy-done.9, f32[1024]{0:T(1024)S(1)} %fusion.199), kind=kOutput, calls=%fused_computation | convolution fusion | flops 25787105280 | bytes 52432896 | tf_op jit(solution)/shard_map/qy,yxl->qxl/dot_general | solution.py:47
  285.5 12.0 copy.86
  306.9 358.0 %all-to-all-done.1 = f32[8,64,64,128]{3,2,1,0:T(8,128)} async-done(((f32[8,64,64,128]{3,2,1,0:T(8,128)}), f32[8,64,64,128]{3,2,1,0:T(8,128)}, u32[]{:S(2)}, u32[]{:S(2)}) %all-to-all-start.1) | async-done | bytes 16777248 | tf_op jit(solution)/shard_map/all_to_all | solution.py:100
  664.9 17.6 copy.46
  682.5 11.1 slice_negate_fusion.5
  693.6 23.7 %maximum_maximum_fusion = f32[1024,64,128]{0,2,1:T(8,128)} fusion(f32[512,64,64]{0,2,1:T(8,128)} %get-tuple-element.22, f32[512,64,64]{0,2,1:T(8,128)} %get-tuple-element.21, f32[512,64,128]{0,2,1:T(8,128)} %copy.46), kind=kLoop, calls=%fused_computation.6 | loop fusion | flops 16777216 | bytes 67108864 | tf_op jit(solution)/shard_map/concatenate | solution.py:38
  717.3 30.4 %fusion.89 = f32[512,8192]{0,1:S(1)} fusion(f32[1024,8192]{0,1:T(8,128)} %bitcast.101, f32[512,1024]{1,0:T(8,128)S(1)} %copy-done.8, f32[1024]{0:T(1024)S(1)} %fusion.199), kind=kOutput, calls=%fused_computation.114 | convolution fusion | flops 25770328064 | bytes 52432896
  760.1 72.5 %select_select_fusion.1 = (f32[512,64,128]{0,2,1:T(8,128)}, f32[512,64,128]{0,2,1:T(8,128)S(1)}) fusion(f32[512,64,128]{0,2,1:T(8,128)} %bitcast.105, f32[]{:T(128)} %bitcast.16, f32[128]{0:T(128)S(1)} %fusion.207, f32[512,64]{0,1:T(8,128)S(1)} %broadcast_add_fusion, f32[512,64]{0,1:T(8,128)S(1)} %get-tuple-element.27, f32[512,64]{0,1:T(8,128)S(1)} %get-tuple-element.25, ...), kind=kLoop, calls=%fused_computation.95 | loop fusion | flops 465567744 | bytes 50987784 | tf_op jit(solution)/shard_map/jit(_where)/select_n | solution.py:140
  840.0 31.7 %fusion.18 = f32[512,64,128]{2,0,1:T(8,128)} fusion(f32[512,1024,1]{1,0,2:T(8,128)S(1)} %copy-done.7, f32[512,64,64]{0,2,1:T(8,128)} %get-tuple-element.14, f32[512,64,64]{0,2,1:T(8,128)} %get-tuple-element.13, f32[512,64,128]{0,2,1:T(8,128)S(1)} %get-tuple-element.6), kind=kOutput, calls=%fused_computation.19 | convolution fusion | flops 25786580992 | bytes 52428800 | tf_op jit(solution)/shard_map/xk,kql->xql/dot_general | solution.py:47
  871.6 11.8 copy.60
  892.7 9.8 slice_negate_fusion.4
  902.4 30.0 %fusion.6 = f32[512,64,128]{2,0,1:T(8,128)S(1)} fusion(f32[512,1024,1]{1,0,2:T(8,128)S(1)} %copy-done.7, f32[512,64,64]{0,2,1:T(8,128)} %get-tuple-element.10, f32[512,64,64]{0,2,1:T(8,128)S(1)} %get-tuple-element.9, f32[512,64,128]{0,2,1:T(8,128)} %get-tuple-element.5), kind=kOutput, calls=%fused_computation.7 | convolution fusion | flops 25786580992 | bytes 52428800 | tf_op jit(solution)/shard_map/xk,kql->xql/dot_general | solution.py:47
  939.0 313.8 %all-to-all-done.4 = f32[8,64,64,128]{3,1,2,0:T(8,128)} async-done(((f32[8,64,64,128]{3,1,2,0:T(8,128)}), f32[8,64,64,128]{3,1,2,0:T(8,128)}, u32[]{:S(2)}, u32[]{:S(2)}) %all-to-all-start.4) | async-done | bytes 16777248 | tf_op jit(solution)/shard_map/all_to_all | solution.py:143
  1252.8 9.5 all-to-all-start.2
  1262.3 11.0 copy.61
  1273.3 12.4 slice_negate_fusion
  1289.7 36.5 %fusion.24 = f32[512,64,128]{2,0,1:T(8,128)} fusion(f32[512,1024,1]{1,0,2:T(8,128)S(1)} %copy-done.6, f32[512,64,64]{2,0,1:T(8,128)} %get-tuple-element.12, f32[512,64,64]{2,0,1:T(8,128)} %get-tuple-element.11, f32[512,64,128]{2,0,1:T(8,128)} %bitcast.99), kind=kOutput, calls=%fused_computation.25 | convolution fusion | flops 25786580992 | bytes 52428800 | tf_op jit(solution)/shard_map/yq,qxl->yxl/dot_general | solution.py:47
  1326.2 11.8 copy.62
  1338.0 284.3 %all-to-all-done.2 = f32[8,64,64,128]{3,1,2,0:T(8,128)} async-done(((f32[8,64,64,128]{3,1,2,0:T(8,128)}), f32[8,64,64,128]{3,1,2,0:T(8,128)}, u32[]{:S(2)}, u32[]{:S(2)}) %all-to-all-start.2) | async-done | bytes 16777248 | tf_op jit(solution)/shard_map/all_to_all | solution.py:143
  1629.9 11.0 copy.56
  1640.9 13.7 slice_negate_fusion.1
  1656.7 36.5 %fusion.12 = f32[512,64,128]{2,0,1:T(8,128)} fusion(f32[512,1024,1]{1,0,2:T(8,128)S(1)} %copy-done.6, f32[512,64,64]{2,0,1:T(8,128)} %get-tuple-element.8, f32[512,64,64]{2,0,1:T(8,128)} %get-tuple-element.7, f32[512,64,128]{2,0,1:T(8,128)} %bitcast.97), kind=kOutput, calls=%fused_computation.13 | convolution fusion | flops 25786580992 | bytes 52428800 | tf_op jit(solution)/shard_map/yq,qxl->yxl/dot_general | solution.py:47
  1693.2 11.7 copy.57
  1704.9 106.6 %all-to-all-done.5 = f32[4,128,64,128]{3,1,2,0:T(8,128)} async-done(((f32[4,128,64,128]{3,1,2,0:T(8,128)}), f32[4,128,64,128]{3,1,2,0:T(8,128)}, u32[]{:S(2)}, u32[]{:S(2)}) %all-to-all-start.5) | async-done | bytes 16777248 | tf_op jit(solution)/shard_map/all_to_all | solution.py:149
  1819.0 18.4 convolution_bitcast_fusion
  1837.4 162.3 %all-to-all-done.3 = f32[4,128,64,128]{3,1,2,0:T(8,128)} async-done(((f32[4,128,64,128]{3,1,2,0:T(8,128)}), f32[4,128,64,128]{3,1,2,0:T(8,128)}, u32[]{:S(2)}, u32[]{:S(2)}) %all-to-all-start.3) | async-done | bytes 16777248 | tf_op jit(solution)/shard_map/all_to_all | solution.py:149
  1999.7 17.4 convolution_bitcast_fusion.1
  2017.2 11.4 pad_maximum_fusion
  (49 shorter events, 71.9 us)
Async XLA Ops:
  18.9 188.6 %all-to-all-start = ((f32[4,128,64,128]{1,3,2,0:T(8,128)}), f32[4,128,64,128]{1,3,2,0:T(8,128)}, u32[]{:S(2)}, u32[]{:S(2)}) async-start(f32[4,128,64,128]{1,3,2,0:T(8,128)} %fusion.84), calls=%async_computation | async-start | bytes 33554432 | tf_op jit(solution)/shard_map/all_to_all | solution.py:96
  225.0 23.7 %copy-start.9 = (f32[512,1024]{1,0:T(8,128)S(1)}, f32[512,1024]{1,0:T(8,128)}, u32[]{:S(2)}) copy-start(f32[512,1024]{1,0:T(8,128)} %constant.174.clone) | copy-start | bytes 6291460
  297.5 7.4 copy-start.5
  297.5 367.5 %all-to-all-start.1 = ((f32[8,64,64,128]{3,2,1,0:T(8,128)}), f32[8,64,64,128]{3,2,1,0:T(8,128)}, u32[]{:S(2)}, u32[]{:S(2)}) async-start(f32[8,64,64,128]{3,2,1,0:T(8,128)} %bitcast.100), calls=%async_computation.1 | async-start | bytes 33554432 | tf_op jit(solution)/shard_map/all_to_all | solution.py:100
  693.6 23.7 %copy-start.8 = (f32[512,1024]{1,0:T(8,128)S(1)}, f32[512,1024]{1,0:T(8,128)}, u32[]{:S(2)}) copy-start(f32[512,1024]{1,0:T(8,128)} %constant.176.clone) | copy-start | bytes 6291460
  747.7 6.2 copy-start.3
  832.7 7.3 copy-start.7
  883.5 369.3 %all-to-all-start.4 = ((f32[8,64,64,128]{3,1,2,0:T(8,128)}), f32[8,64,64,128]{3,1,2,0:T(8,128)}, u32[]{:S(2)}, u32[]{:S(2)}) async-start(f32[8,64,64,128]{3,1,2,0:T(8,128)} %copy.60), calls=%async_computation.4 | async-start | bytes 33554432 | tf_op jit(solution)/shard_map/all_to_all | solution.py:143
  1252.8 369.6 %all-to-all-start.2 = ((f32[8,64,64,128]{3,1,2,0:T(8,128)}), f32[8,64,64,128]{3,1,2,0:T(8,128)}, u32[]{:S(2)}, u32[]{:S(2)}) async-start(f32[8,64,64,128]{3,1,2,0:T(8,128)} %copy.55), calls=%async_computation.2 | async-start | bytes 33554432 | tf_op jit(solution)/shard_map/all_to_all | solution.py:143
  1273.3 16.4 copy-start.1
  1273.3 16.4 copy-start.6
  1622.4 189.1 %all-to-all-start.5 = ((f32[4,128,64,128]{3,1,2,0:T(8,128)}), f32[4,128,64,128]{3,1,2,0:T(8,128)}, u32[]{:S(2)}, u32[]{:S(2)}) async-start(f32[4,128,64,128]{3,1,2,0:T(8,128)} %copy.62), calls=%async_computation.5 | async-start | bytes 33554432 | tf_op jit(solution)/shard_map/all_to_all | solution.py:149
  1640.9 15.9 copy-start
  1704.9 114.1 %copy-start.4 = (f32[4,128,512,1]{2,1,3,0:T(8,128)S(1)}, f32[4,128,512,1]{2,1,3,0:T(8,128)}, u32[]{:S(2)}) copy-start(f32[4,128,512,1]{2,1,3,0:T(8,128)} %constant.181) | copy-start | bytes 3145732
  1811.5 188.3 %all-to-all-start.3 = ((f32[4,128,64,128]{3,1,2,0:T(8,128)}), f32[4,128,64,128]{3,1,2,0:T(8,128)}, u32[]{:S(2)}, u32[]{:S(2)}) async-start(f32[4,128,64,128]{3,1,2,0:T(8,128)} %copy.57), calls=%async_computation.3 | async-start | bytes 33554432 | tf_op jit(solution)/shard_map/all_to_all | solution.py:149
  1999.7 17.5 copy-start.2
where the time goes:
time: 2040 us; the launch traced here: 2030 us
  waiting for transfers between devices  1410 us (69%)
  matrix products  257 us (13%)
  other arithmetic  188 us (9%)
  local copies, waits for them, and re-layouts  127 us (6%)
  starting transfers between devices  48.3 us (2%)
    all_to_all x2, waiting for transfers between devices, per_device(): lax.all_to_all(field, 'gx', split_axis=0, concat_axis=0, tiled=True)  598 us
    all_to_all x1, waiting for transfers between devices, per_device(): lax.all_to_all(values, 'gx', split_axis=0, concat_axis=0, tiled=True)  358 us
    all_to_all x2, waiting for transfers between devices, per_device(): field = lax.all_to_all(field, 'gy', split_axis=0, concat_axis=0, tiled=True)  269 us
    dot_general x8, matrix products, dot(): jnp.einsum(spec, left, right, precision=PREC, preferred_element_type=jnp....  226 us
    all_to_all x1, waiting for transfers between devices, per_device(): lax.all_to_all(values, 'gy', split_axis=0, concat_axis=0, tiled=True)  181 us
    neg x6, other arithmetic, times_i(): return jnp.concatenate([-values[..., half:], values[..., :half]], -1)  78 us
    select_n x1, other arithmetic, per_device(): field = jnp.where(first & (lane == half), fix_im[:, :, None], field)  72.5 us
  transfers between devices with their start and end apart: 6, of which 6 were waited for; matrix products, arithmetic and copies ran while one was open for 10% of the time, Pallas kernels for 0%

commit v1 on v0

v1 whole, which is shorter than its diff:
```python
import functools
import math

import jax
import jax.numpy as jnp
import numpy as np
from jax import lax
from jax.experimental import pallas as pl
from jax.experimental.pallas import tpu as pltpu
from jax.sharding import PartitionSpec as P

MESH = pl.DeviceIdType.MESH
STEP = 8
PIECE = 16
VMEM = 63 * 1024 * 1024


def window(k_squared, scale_squared):
    u_squared = k_squared * scale_squared
    u_value = jnp.sqrt(u_squared)
    is_small = u_value < 0.2
    safe = jnp.where(is_small, 1.0, u_value)
    turns = jnp.floor(safe * (1.0 / math.pi) + 0.5)
    rest = safe - turns * 3.140625
    rest = rest - turns * 9.67502593994140625e-4
    rest = rest - turns * 1.509957990978376432e-7
    s2 = rest * rest
    sin_v = rest * (1.0 + s2 * (-1.6666666666e-1 + s2 * (8.3333333e-3 + s2 * (
        -1.98412698e-4 + s2 * (2.75573192e-6 + s2 * -2.50521084e-8)))))
    cos_v = 1.0 + s2 * (-0.5 + s2 * (4.16666666e-2 + s2 * (-1.38888889e-3 + s2 * (
        2.48015873e-5 + s2 * (-2.75573192e-7 + s2 * 2.08767570e-9)))))
    half = turns * 0.5
    sign = jnp.where(half == jnp.floor(half), 3.0, -3.0)
    closed = sign * (sin_v - safe * cos_v) / (safe * safe * safe)
    series = 1.0 - u_squared / 10.0 + u_squared * u_squared / 280.0
    return jnp.where(is_small, series, closed)


def basis(length, order):
    freq = np.array([length // 2 if s and f == 0 else f for f, s in order])
    sine = np.array([s and f > 0 for f, s in order])
    angle = 2.0 * math.pi / length * (np.outer(freq, np.arange(length)) % length)
    table = np.where(sine[:, None], np.sin(angle), np.cos(angle))
    gain = np.where((freq == 0) | (freq == length // 2), 1.0, 2.0) / length
    return table, gain[:, None]


def blocked(length, parts):
    width = length // 2 // parts
    return [(p * width + j, s) for p in range(parts) for s in (0, 1) for j in range(width)]


def paired(length):
    return [(f, s) for f in range(length // 2) for s in (0, 1)]


def tripled(table, axis):
    table = jnp.asarray(table, jnp.float32)
    high = table.astype(jnp.bfloat16)
    low = (table - high.astype(jnp.float32)).astype(jnp.bfloat16)
    return jnp.concatenate([high, low, high], axis)


def split(values, axis):
    high = values.astype(jnp.bfloat16)
    low = (values - high.astype(jnp.float32)).astype(jnp.bfloat16)
    return jnp.concatenate([high, high, low], axis)


def product(matrix, columns):
    width = columns[0].shape[1]
    if width % 128:
        return [jnp.dot(matrix, split(c, 0), preferred_element_type=jnp.float32) for c in columns]
    out = jnp.dot(matrix, split(jnp.concatenate(columns, 1), 0), preferred_element_type=jnp.float32)
    return [out[:, i * width:(i + 1) * width] for i in range(len(columns))]


def greet(count_gx, count_gy, me, my):
    barrier = pltpu.get_barrier_semaphore()
    for s in range(1, count_gx):
        pl.semaphore_signal(barrier, inc=1, device_id={"gx": lax.rem(me + s, count_gx)}, device_id_type=MESH)
    for s in range(1, count_gy):
        pl.semaphore_signal(barrier, inc=1, device_id={"gy": lax.rem(my + s, count_gy)}, device_id_type=MESH)
    pl.semaphore_wait(barrier, count_gx + count_gy - 2)


def forward_kernel(count_gx, count_gy, density, fwd_z, fwd_y, cube, loaded, packed, lines, planes,
                   load_sem, z_send, z_recv, x_send, x_recv):
    rows_x, rows_y, length = density.shape
    lanes = length // count_gy
    cols = length // count_gx
    steps = rows_x // STEP
    me, my = lax.axis_index("gx"), lax.axis_index("gy")

    def load(i):
        return pltpu.make_async_copy(
            density.at[pl.ds(i * STEP, STEP)], loaded.at[lax.rem(i, 2)], load_sem.at[lax.rem(i, 2)])

    def z_part(i, s, source):
        return pltpu.make_async_remote_copy(
            src_ref=packed.at[i, lax.rem(my + s, count_gy)],
            dst_ref=lines.at[pl.ds(i * STEP, STEP), pl.ds(source * rows_y, rows_y)],
            send_sem=z_send.at[i, s], recv_sem=z_recv.at[i, s],
            device_id={"gy": lax.rem(my + s, count_gy)}, device_id_type=MESH)

    def z_own(i):
        return pltpu.make_async_copy(
            packed.at[i, my], lines.at[pl.ds(i * STEP, STEP), pl.ds(my * rows_y, rows_y)], z_send.at[i, 0])

    def x_part(i, s, source):
        return pltpu.make_async_remote_copy(
            src_ref=planes.at[pl.ds(i * STEP, STEP), pl.ds(lax.rem(me + s, count_gx) * cols, cols)],
            dst_ref=cube.at[pl.ds(source * rows_x + i * STEP, STEP)],
            send_sem=x_send.at[i, s], recv_sem=x_recv.at[i, s],
            device_id={"gx": lax.rem(me + s, count_gx)}, device_id_type=MESH)

    def x_own(i):
        return pltpu.make_async_copy(
            planes.at[pl.ds(i * STEP, STEP), pl.ds(me * cols, cols)],
            cube.at[pl.ds(me * rows_x + i * STEP, STEP)], x_send.at[i, 0])

    load(0).start()
    greet(count_gx, count_gy, me, my)

    def along_z(i, _):
        @pl.when(i + 1 < steps)
        def _():
            load(i + 1).start()
        load(i).wait()

        def pair(j, _):
            rows = loaded[lax.rem(i, 2), pl.ds(2 * j, 2)].reshape(2 * rows_y, length)
            out = jnp.dot(split(rows, 1), fwd_z[...], preferred_element_type=jnp.float32)
            for b in range(count_gy):
                packed[i, b, pl.ds(2 * j, 2)] = out[:, b * lanes:(b + 1) * lanes].reshape(2, rows_y, lanes)
            return 0

        lax.fori_loop(0, STEP // 2, pair, 0)
        for s in range(1, count_gy):
            z_part(i, s, my).start()
        z_own(i).start()
        return 0

    lax.fori_loop(0, steps, along_z, 0)

    def along_y(i, _):
        for s in range(1, count_gy):
            z_part(i, s, lax.rem(my + count_gy - s, count_gy)).wait_recv()
        z_own(i).wait()

        def pair(j, _):
            row = i * STEP + 2 * j
            out = product(fwd_y[...], [lines[row], lines[row + 1]])
            planes[row] = out[0]
            planes[row + 1] = out[1]
            return 0

        lax.fori_loop(0, STEP // 2, pair, 0)
        for s in range(1, count_gx):
            x_part(i, s, me).start()
        x_own(i).start()
        return 0

    lax.fori_loop(0, steps, along_y, 0)

    def finish(i, _):
        for s in range(1, count_gy):
            z_part(i, s, my).wait_send()
        for s in range(1, count_gx):
            x_part(i, s, me).wait_send()
            x_part(i, s, lax.rem(me + count_gx - s, count_gx)).wait_recv()
        x_own(i).wait()
        return 0

    lax.fori_loop(0, steps, finish, 0)


def inverse_kernel(count_gx, count_gy, rows_x, rows_y, scales, cube, fwd_x, inv_x, inv_y,
                   early, late, result, loaded, first, second, lines, planes,
                   load_sem, a_send, a_recv, b_send, b_recv, line_sem, z_send, z_recv):
    length, cols, lanes = cube.shape
    pieces = cols // PIECE
    steps = rows_x // STEP
    mid = length // 2
    me, my = lax.axis_index("gx"), lax.axis_index("gy")
    slots = planes.shape[0]

    def load(c):
        return pltpu.make_async_copy(
            cube.at[:, pl.ds(c * PIECE, PIECE)], loaded.at[lax.rem(c, 2)], load_sem.at[lax.rem(c, 2)])

    def a_part(c, s, source):
        return pltpu.make_async_remote_copy(
            src_ref=first.at[c, pl.ds(lax.rem(me + s, count_gx) * rows_x, rows_x)],
            dst_ref=early.at[:, pl.ds(source * cols + c * PIECE, PIECE)],
            send_sem=a_send.at[c, s], recv_sem=a_recv.at[c, s],
            device_id={"gx": lax.rem(me + s, count_gx)}, device_id_type=MESH)

    def a_own(c):
        return pltpu.make_async_copy(
            first.at[c, pl.ds(me * rows_x, rows_x)],
            early.at[:, pl.ds(me * cols + c * PIECE, PIECE)], a_send.at[c, 0])

    def b_part(i, s, source):
        return pltpu.make_async_remote_copy(
            src_ref=second.at[pl.ds(lax.rem(me + s, count_gx) * rows_x + i * STEP, STEP)],
            dst_ref=late.at[pl.ds(i * STEP, STEP), pl.ds(source * cols, cols)],
            send_sem=b_send.at[i, s], recv_sem=b_recv.at[i, s],
            device_id={"gx": lax.rem(me + s, count_gx)}, device_id_type=MESH)

    def b_own(i):
        return pltpu.make_async_copy(
            second.at[pl.ds(me * rows_x + i * STEP, STEP)],
            late.at[pl.ds(i * STEP, STEP), pl.ds(me * cols, cols)], b_send.at[i, 0])

    def z_part(n, s, source):
        slot = lax.rem(n, slots)
        r, i = n // steps, lax.rem(n, steps)
        return pltpu.make_async_remote_copy(
            src_ref=planes.at[slot, :, pl.ds(lax.rem(my + s, count_gy) * rows_y, rows_y)],
            dst_ref=result.at[r, source, pl.ds(i * STEP, STEP)],
            send_sem=z_send.at[n, s], recv_sem=z_recv.at[n, s],
            device_id={"gy": lax.rem(my + s, count_gy)}, device_id_type=MESH)

    def z_own(n):
        slot = lax.rem(n, slots)
        r, i = n // steps, lax.rem(n, steps)
        return pltpu.make_async_copy(
            planes.at[slot, :, pl.ds(my * rows_y, rows_y)],
            result.at[r, my, pl.ds(i * STEP, STEP)], z_send.at[n, 0])

    load(0).start()
    greet(count_gx, count_gy, me, my)

    kx = lax.broadcasted_iota(jnp.int32, (mid, lanes), 0)
    top = kx == 0
    kx_sq = (kx * kx).astype(jnp.float32)
    lane = lax.broadcasted_iota(jnp.int32, (mid, lanes), 1)
    kz = my * (lanes // 2) + jnp.where(lane < lanes // 2, lane, lane - lanes // 2)
    kz = jnp.where((kz == 0) & (lane >= lanes // 2), mid, kz)
    kz_sq = (kz * kz).astype(jnp.float32)
    far_sq = jnp.where(top, float(mid) ** 2, kx_sq)

    second_rows = second.reshape(length * cols, lanes)

    def along_x(c, _):
        @pl.when(c + 1 < pieces)
        def _():
            load(c + 1).start()
        load(c).wait()
        source = loaded.at[lax.rem(c, 2)].reshape(length * PIECE, lanes)
        target = first.at[c].reshape(length * PIECE, lanes)

        def pair(j, _):
            columns = [source[pl.ds(2 * j + k, length, stride=PIECE), :] for k in range(2)]
            spectrum = product(fwd_x[...], columns)
            freq = me * (cols // 2) + c * (PIECE // 2) + j
            sine_freq = jnp.where(freq == 0, mid, freq)
            plain = [(freq * freq).astype(jnp.float32), (sine_freq * sine_freq).astype(jnp.float32)]
            for r in range(2):
                scale = scales[r]
                weighted = []
                common = window(kx_sq + plain[0] + kz_sq, scale)
                weights = []
                for k in range(2):
                    edge = window(float(mid) ** 2 + plain[k] + kz_sq[:8], scale)
                    if k == 0:
                        cosine = common
                    else:
                        cosine = window(kx_sq + plain[1] + kz_sq, scale)
                    sine = jnp.concatenate([jnp.where(top[:8], edge, cosine[:8]), cosine[8:]], 0)
                    weighted.append(spectrum[k] * jnp.concatenate([cosine, sine], 0))
                out = product(inv_x[...], weighted)
                for k in range(2):
                    if r == 0:
                        target[pl.ds(2 * j + k, length, stride=PIECE), :] = out[k]
                    else:
                        second_rows[pl.ds(c * PIECE + 2 * j + k, length, stride=cols), :] = out[k]
            return 0

        lax.fori_loop(0, PIECE // 2, pair, 0)
        for s in range(1, count_gx):
            a_part(c, s, me).start()
        a_own(c).start()
        return 0

    lax.fori_loop(0, pieces, along_x, 0)

    def send_second(i, _):
        for s in range(1, count_gx):
            b_part(i, s, me).start()
        b_own(i).start()
        return 0

    lax.fori_loop(0, steps, send_second, 0)

    def along_y(n, bring):
        @pl.when(n >= slots)
        def _():
            for s in range(1, count_gy):
                z_part(n - slots, s, my).wait_send()
            z_own(n - slots).wait()
        bring.start()
        bring.wait()
        slot = lax.rem(n, slots)

        def pair(j, _):
            out = product(inv_y[...], [lines[2 * j], lines[2 * j + 1]])
            planes[slot, 2 * j] = out[0]
            planes[slot, 2 * j + 1] = out[1]
            return 0

        lax.fori_loop(0, STEP // 2, pair, 0)
        for s in range(1, count_gy):
            z_part(n, s, my).start()
        z_own(n).start()

    def wait_first(c, _):
        for s in range(1, count_gx):
            a_part(c, s, lax.rem(me + count_gx - s, count_gx)).wait_recv()
        a_own(c).wait()
        return 0

    lax.fori_loop(0, pieces, wait_first, 0)

    def first_rows(i, _):
        along_y(i, pltpu.make_async_copy(early.at[pl.ds(i * STEP, STEP)], lines, line_sem))
        return 0

    lax.fori_loop(0, steps, first_rows, 0)

    def later_rows(i, _):
        for s in range(1, count_gx):
            b_part(i, s, lax.rem(me + count_gx - s, count_gx)).wait_recv()
        b_own(i).wait()
        along_y(steps + i, pltpu.make_async_copy(late.at[pl.ds(i * STEP, STEP)], lines, line_sem))
        return 0

    lax.fori_loop(0, steps, later_rows, 0)

    def drain_a(c, _):
        for s in range(1, count_gx):
            a_part(c, s, me).wait_send()
        return 0

    lax.fori_loop(0, pieces, drain_a, 0)

    def drain_b(i, _):
        for s in range(1, count_gx):
            b_part(i, s, me).wait_send()
        return 0

    lax.fori_loop(0, steps, drain_b, 0)

    def drain_sends(n, _):
        for s in range(1, count_gy):
            z_part(n, s, my).wait_send()
        z_own(n).wait()
        return 0

    lax.fori_loop(max(0, 2 * steps - slots), 2 * steps, drain_sends, 0)

    def drain_z(n, _):
        for s in range(1, count_gy):
            z_part(n, s, lax.rem(my + count_gy - s, count_gy)).wait_recv()
        return 0

    lax.fori_loop(0, 2 * steps, drain_z, 0)


def per_device(density, radius_cells):
    rows_x, rows_y, length = density.shape
    count_gx = lax.axis_size("gx")
    count_gy = lax.axis_size("gy")
    lanes = length // count_gy
    cols = length // count_gx
    steps = rows_x // STEP
    f32 = jnp.float32
    vmem = pl.BlockSpec(memory_space=pltpu.VMEM)
    hbm = pl.BlockSpec(memory_space=pl.ANY)
    dma = pltpu.SemaphoreType.DMA

    table_z, gain_z = basis(length, blocked(length, count_gy))
    table_y, gain_y = basis(length, paired(length))
    table_x, gain_x = basis(length, blocked(length, 1))
    flops = 2 * 3 * rows_x * rows_y * length * length

    cube = pl.pallas_call(
        functools.partial(forward_kernel, count_gx, count_gy),
        out_shape=jax.ShapeDtypeStruct((length, cols, lanes), f32),
        in_specs=[hbm, vmem, vmem],
        out_specs=hbm,
        scratch_shapes=[
            pltpu.VMEM((2, STEP, rows_y, length), f32),
            pltpu.VMEM((steps, count_gy, STEP, rows_y, lanes), f32),
            pltpu.VMEM((rows_x, length, lanes), f32),
            pltpu.VMEM((rows_x, length, lanes), f32),
            dma((2,)), dma((steps, count_gy)), dma((steps, count_gy)),
            dma((steps, count_gx)), dma((steps, count_gx)),
        ],
        compiler_params=pltpu.CompilerParams(
            collective_id=0, has_side_effects=True, vmem_limit_bytes=VMEM),
        cost_estimate=pl.CostEstimate(flops=2 * flops, bytes_accessed=8 * density.size, transcendentals=0),
        name="forward",
    )(density, tripled(table_z.T, 0), tripled(table_y, 1))

    scales = 2.0 * math.pi / length * radius_cells.astype(f32)
    pieces = cols // PIECE
    slots = 4
    field = jax.ShapeDtypeStruct((rows_x, length, lanes), f32)
    _, _, fields = pl.pallas_call(
        functools.partial(inverse_kernel, count_gx, count_gy, rows_x, rows_y),
        out_shape=(field, field, jax.ShapeDtypeStruct((2, count_gy, rows_x, rows_y, lanes), f32)),
        in_specs=[pl.BlockSpec(memory_space=pltpu.SMEM), hbm, vmem, vmem, vmem],
        out_specs=(hbm, hbm, hbm),
        scratch_shapes=[
            pltpu.VMEM((2, length, PIECE, lanes), f32),
            pltpu.VMEM((pieces, length, PIECE, lanes), f32),
            pltpu.VMEM((length, cols, lanes), f32),
            pltpu.VMEM((STEP, length, lanes), f32),
            pltpu.VMEM((slots, STEP, length, lanes), f32),
            dma((2,)), dma((pieces, count_gx)), dma((pieces, count_gx)),
            dma((steps, count_gx)), dma((steps, count_gx)), dma(()),
            dma((2 * steps, count_gy)), dma((2 * steps, count_gy)),
        ],
        compiler_params=pltpu.CompilerParams(
            collective_id=1, has_side_effects=True, vmem_limit_bytes=VMEM),
        cost_estimate=pl.CostEstimate(flops=5 * flops, bytes_accessed=20 * density.size, transcendentals=0),
        name="inverse",
    )(scales * scales, cube, tripled(table_x, 1), tripled((table_x * gain_x).T, 1), tripled((table_y * gain_y).T, 1))

    inv_z = jnp.asarray(table_z * gain_z, f32).reshape(count_gy, lanes, length)
    return jnp.einsum("rgxyl,glz->rxyz", fields, inv_z,
                      precision=lax.Precision.HIGH, preferred_element_type=f32)


def solution(mesh):
    return jax.shard_map(
        per_device,
        mesh=mesh,
        in_specs=(P("gx", "gy", None), P()),
        out_specs=P(None, "gx", "gy", None),
        check_vma=False,
    )
```

time: 2040 us -> 1340 us (0.66)
  waiting for transfers between devices: 1410 us -> 0 us
  Pallas kernels: 0 us -> 1300 us
  matrix products: 257 us -> 33.2 us
  other arithmetic: 188 us -> 1.17 us
  local copies, waits for them, and re-layouts: 127 us -> 0 us
  starting transfers between devices: 48.3 us -> 0 us
    all_to_all x6 -> x0, waiting for transfers between devices: 1410 us -> none  [the longest x2 598 us: per_device(): lax.all_to_all(field, 'gx', split_axis=0, concat_axis=0, tiled=True)]
    pallas_call x0 -> x2, Pallas kernels: none -> 1300 us  [the longest x1 907 us: per_device(): pl.pallas_call(functools.partial(inverse_kernel, count_gx, count_gy, rows...]
    dot_general x8 -> x1, matrix products: 226 us -> 33.2 us  [per_device(): jnp.einsum('rgxyl,glz->rxyz', fields, inv_z, precision=lax.Precision.HIGH...]
    reshape x7 -> x0, local copies, waits for them, and re-layouts: 88.9 us -> none  [the longest x2 23.5 us: per_device(): field = field.reshape(count_gy, rows_y, rows_x, lanes)]
    neg x6 -> x0, other arithmetic: 78 us -> none  [times_i(): return jnp.concatenate([-values[..., half:], values[..., :half]], -1)]
    select_n x2 -> x0, other arithmetic: 72.5 us -> none  [the longest x1 72.5 us: per_device(): field = jnp.where(first & (lane == half), fix_im[:, :, None], field)]
    all_to_all x6 -> x0, starting transfers between devices: 48.3 us -> none  [the longest x2 18.7 us: per_device(): lax.all_to_all(field, 'gx', split_axis=0, concat_axis=0, tiled=True)]
    unnamed x1 -> x0, matrix products: 30.4 us -> none
  transfers between devices with their start and end apart: 6 -> 0, of which waited for: 6 -> 0; matrix products, arithmetic and copies ran while one was open for 10% -> 0% of each run, Pallas kernels for 0% -> 0%
where the time goes in v1:
time: 1340 us
  Pallas kernels  1300 us (97%)
  matrix products  33.2 us (2%)
    pallas_call x1, Pallas kernels, per_device(): pl.pallas_call(functools.partial(inverse_kernel, count_gx, count_gy, rows...  907 us
    pallas_call x1, Pallas kernels, per_device(): pl.pallas_call(functools.partial(forward_kernel, count_gx, count_gy), out...  397 us
    dot_general x1, matrix products, per_device(): jnp.einsum('rgxyl,glz->rxyz', fields, inv_z, precision=lax.Precision.HIGH...  33.2 us

profile of v1, /device:TPU:11, one launch (start us, length us, event | category | flops | bytes accessed | tf_op | source)
XLA Modules:
  0.0 1338.3 jit_solution(6482575100811358471)
XLA Ops:
  0.0 1.2 multiply_multiply_fusion.scales
  1.2 396.5 %forward.1.cube = f32[512,64,128]{2,1,0:T(8,128)} custom-call(f32[64,128,512]{2,1,0:T(8,128)} %density.1, bf16[1536,512]{1,0:T(8,128)(2,1)} %constant.24.fwd_z, bf16[512,1536]{1,0:T(8,128)(2,1)} %constant.29.fwd_y), custom_call_target="tpu_custom_call" | custom-call | flops 25769803776 | bytes 33554432 | tf_op jit(solution)/shard_map/forward/pallas_call | solution.py:388
  397.7 907.3 %inverse.1 = (f32[64,512,128]{2,1,0:T(8,128)}, f32[64,512,128]{2,1,0:T(8,128)}, f32[2,4,64,128,128]{4,3,2,1,0:T(8,128)}) custom-call(f32[2]{0:T(128)} %multiply_multiply_fusion.scales, f32[512,64,128]{2,1,0:T(8,128)} %forward.1.cube, bf16[512,1536]{1,0:T(8,128)(2,1)} %constant.34.fwd_x, bf16[512,1536]{1,0:T(8,128)(2,1)} %constant.39.inv_x, ...), custom_call_target="tpu_custom_call" | custom-call | flops 64424509440 | bytes 83886080 | tf_op jit(solution)/shard_map/inverse/pallas_call | solution.py:411
  1305.1 33.2 %convolution_bitcast_fusion = f32[2,64,128,512]{3,2,1,0:T(8,128)} fusion(f32[2,4,64,128,128]{4,3,2,1,0:T(8,128)} %get-tuple-element.6, f32[4,128,512,1,1]{2,1,0,4,3:T(8,128)} %constant.46), kind=kOutput, calls=%fused_computation | convolution fusion | flops 25769803776 | bytes 68157440 | tf_op jit(solution)/shard_map/rgxyl,glz->rxyz/dot_general | solution.py:433

commit v2 on v1

v2 whole, which is shorter than its diff:
```python
import functools
import math

import jax
import jax.numpy as jnp
import numpy as np
from jax import lax
from jax.experimental import pallas as pl
from jax.experimental.pallas import tpu as pltpu
from jax.sharding import PartitionSpec as P

MESH = pl.DeviceIdType.MESH
STEP = 8
PIECE = 8
VMEM = 63 * 1024 * 1024


def window(k_squared, scale_squared):
    u_squared = k_squared * scale_squared
    u_value = jnp.sqrt(u_squared)
    is_small = u_value < 0.2
    safe = jnp.where(is_small, 1.0, u_value)
    turns = jnp.floor(safe * (1.0 / math.pi) + 0.5)
    rest = safe - turns * 3.140625
    rest = rest - turns * 9.67502593994140625e-4
    rest = rest - turns * 1.509957990978376432e-7
    s2 = rest * rest
    sin_v = rest * (1.0 + s2 * (-1.6666666666e-1 + s2 * (8.3333333e-3 + s2 * (
        -1.98412698e-4 + s2 * (2.75573192e-6 + s2 * -2.50521084e-8)))))
    cos_v = 1.0 + s2 * (-0.5 + s2 * (4.16666666e-2 + s2 * (-1.38888889e-3 + s2 * (
        2.48015873e-5 + s2 * (-2.75573192e-7 + s2 * 2.08767570e-9)))))
    half = turns * 0.5
    sign = jnp.where(half == jnp.floor(half), 3.0, -3.0)
    closed = sign * (sin_v - safe * cos_v) / (safe * safe * safe)
    series = 1.0 - u_squared / 10.0 + u_squared * u_squared / 280.0
    return jnp.where(is_small, series, closed)


def basis(length, order):
    freq = np.array([length // 2 if s and f == 0 else f for f, s in order])
    sine = np.array([s and f > 0 for f, s in order])
    angle = 2.0 * math.pi / length * (np.outer(freq, np.arange(length)) % length)
    table = np.where(sine[:, None], np.sin(angle), np.cos(angle))
    gain = np.where((freq == 0) | (freq == length // 2), 1.0, 2.0) / length
    return table, gain[:, None]


def blocked(length, parts):
    width = length // 2 // parts
    return [(p * width + j, s) for p in range(parts) for s in (0, 1) for j in range(width)]


def paired(length):
    return [(f, s) for f in range(length // 2) for s in (0, 1)]


def tripled(table, axis):
    table = jnp.asarray(table, jnp.float32)
    high = table.astype(jnp.bfloat16)
    low = (table - high.astype(jnp.float32)).astype(jnp.bfloat16)
    return jnp.concatenate([high, low, high], axis)


def split(values, axis):
    high = values.astype(jnp.bfloat16)
    low = (values - high.astype(jnp.float32)).astype(jnp.bfloat16)
    return jnp.concatenate([high, high, low], axis)


def product(matrix, columns):
    width = columns[0].shape[1]
    if width % 128:
        return [jnp.dot(matrix, split(c, 0), preferred_element_type=jnp.float32) for c in columns]
    out = jnp.dot(matrix, split(jnp.concatenate(columns, 1), 0), preferred_element_type=jnp.float32)
    return [out[:, i * width:(i + 1) * width] for i in range(len(columns))]


def group_columns(length, count_gx):
    cols = length // count_gx
    full = (cols * 5 // 8 + PIECE - 1) // PIECE * PIECE
    return full, 2 * (cols - full)


class Line:
    def __init__(self, count):
        self.count = count
        self.half = count // 2
        self.me = lax.axis_index("gx")
        self.side = self.me // self.half
        self.pos = self.place(self.side, self.me)
        self.inner = self.pos < self.half // 2

    def place(self, side, index):
        return side * (index - self.half) + (1 - side) * (self.half - 1 - index)

    def near(self, s):
        pos = lax.rem(self.pos + s, self.half)
        return pos, self.index(self.side, pos)

    def far(self, s):
        pos = lax.rem(self.pos + s, self.half)
        return pos, self.index(1 - self.side, pos)

    def index(self, side, pos):
        return side * (self.half + pos) + (1 - side) * (self.half - 1 - pos)


def greet(count_gx, count_gy, me, my):
    barrier = pltpu.get_barrier_semaphore()
    for s in range(1, count_gx):
        pl.semaphore_signal(barrier, inc=1, device_id={"gx": lax.rem(me + s, count_gx)}, device_id_type=MESH)
    for s in range(1, count_gy):
        pl.semaphore_signal(barrier, inc=1, device_id={"gy": lax.rem(my + s, count_gy)}, device_id_type=MESH)
    pl.semaphore_wait(barrier, count_gx + count_gy - 2)


def loop(low, high, body):
    def step(i, _):
        body(i)
        return 0
    lax.fori_loop(low, high, step, 0)


def remote(src, dst, send, recv, axis, target):
    return pltpu.make_async_remote_copy(
        src_ref=src, dst_ref=dst, send_sem=send, recv_sem=recv,
        device_id={axis: target}, device_id_type=MESH)


def forward_kernel(count_gx, count_gy, density, fwd_z, fwd_y, cube, loaded, packed, lines, planes,
                   load_sem, z_send, z_recv, near_send, near_recv, far_send, far_recv, own_sem):
    rows_x, rows_y, length = density.shape
    lanes = length // count_gy
    full, shared = group_columns(length, count_gx)
    steps = rows_x // STEP
    line = Line(count_gx)
    me, half = line.me, line.half
    my = lax.axis_index("gy")
    groups = ((0, full), (full, shared))

    def load(i):
        return pltpu.make_async_copy(
            density.at[pl.ds(i * STEP, STEP)], loaded.at[lax.rem(i, 2)], load_sem.at[lax.rem(i, 2)])

    def z_part(i, s, source):
        target = lax.rem(my + s, count_gy)
        return remote(packed.at[i, target], lines.at[pl.ds(i * STEP, STEP), pl.ds(source * rows_y, rows_y)],
                      z_send.at[i, s], z_recv.at[i, s], "gy", target)

    def z_own(i):
        return pltpu.make_async_copy(
            packed.at[i, my], lines.at[pl.ds(i * STEP, STEP), pl.ds(my * rows_y, rows_y)], z_send.at[i, 0])

    def columns(i, group, pos, index):
        start = index * full if group == 0 else count_gx * full + pos * shared
        return planes.at[pl.ds(i * STEP, STEP), pl.ds(start, groups[group][1])]

    def landing(i, group, source):
        return cube.at[pl.ds(source * rows_x + i * STEP, STEP), pl.ds(*groups[group])]

    def near_part(i, group, s, source):
        pos, index = line.near(s)
        return remote(columns(i, group, pos, index), landing(i, group, source),
                      near_send.at[i, group, s], near_recv.at[i, group, s], "gx", index)

    def far_part(i, group, s, source):
        pos, index = line.far(s)
        return remote(columns(i, group, pos, index), landing(i, group, source),
                      far_send.at[i, group, s], far_recv.at[i, group, s], "gx", index)

    def own_part(i, group):
        return pltpu.make_async_copy(columns(i, group, line.pos, me), landing(i, group, me), own_sem.at[i, group])

    def send_far(i):
        for group in range(2):
            for s in range(half):
                far_part(i, group, s, me).start()

    load(0).start()
    greet(count_gx, count_gy, me, my)

    def along_z(i):
        @pl.when(i + 1 < steps)
        def _():
            load(i + 1).start()
        load(i).wait()

        def pair(j):
            rows = loaded[lax.rem(i, 2), pl.ds(2 * j, 2)].reshape(2 * rows_y, length)
            out = jnp.dot(split(rows, 1), fwd_z[...], preferred_element_type=jnp.float32)
            for b in range(count_gy):
                packed[i, b, pl.ds(2 * j, 2)] = out[:, b * lanes:(b + 1) * lanes].reshape(2, rows_y, lanes)

        loop(0, STEP // 2, pair)
        for s in range(1, count_gy):
            z_part(i, s, my).start()
        z_own(i).start()

    loop(0, steps, along_z)

    def along_y(i):
        for s in range(1, count_gy):
            z_part(i, s, lax.rem(my + count_gy - s, count_gy)).wait_recv()
        z_own(i).wait()

        def pair(j):
            row = i * STEP + 2 * j
            out = product(fwd_y[...], [lines[row], lines[row + 1]])
            planes[row] = out[0]
            planes[row + 1] = out[1]

        loop(0, STEP // 2, pair)

        @pl.when(line.inner)
        def _():
            send_far(i)
        for group in range(2):
            for s in range(1, half):
                near_part(i, group, s, me).start()
            own_part(i, group).start()

    loop(0, steps, along_y)

    @pl.when(jnp.logical_not(line.inner))
    def _():
        loop(0, steps, send_far)

    def finish(i):
        for s in range(1, count_gy):
            z_part(i, s, my).wait_send()
        for group in range(2):
            for s in range(1, half):
                near_part(i, group, s, me).wait_send()
                source = line.index(line.side, lax.rem(line.pos + half - s, half))
                near_part(i, group, s, source).wait_recv()
            for s in range(half):
                far_part(i, group, s, me).wait_send()
                source = line.index(1 - line.side, lax.rem(line.pos + half - s, half))
                far_part(i, group, s, source).wait_recv()
            own_part(i, group).wait()

    loop(0, steps, finish)


def inverse_kernel(count_gx, count_gy, rows_x, rows_y, scales, cube, fwd_x, inv_x, inv_y,
                   early, late, result, loaded, weights, full_a, shared_a, full_b, shared_b, lines, planes,
                   load_sem, a_send, a_recv, a_own, s_send, s_recv, s_own, ac_send, ac_recv, ax_send, ax_recv,
                   b_send, b_recv, b_own, bf_send, bf_recv, line_sem, z_send, z_recv):
    length, _, lanes = cube.shape
    full, shared = group_columns(length, count_gx)
    count_f, count_s = full // PIECE, shared // PIECE
    steps = rows_x // STEP
    mid = length // 2
    line = Line(count_gx)
    me, half = line.me, line.half
    my = lax.axis_index("gy")
    slots = planes.shape[0]
    low = count_gx * full

    def load(group, c, slot):
        return pltpu.make_async_copy(
            cube.at[:, pl.ds((0 if group == 0 else full) + c * PIECE, PIECE)], loaded.at[slot], load_sem.at[slot])

    def rows_for(group, index, pos, i, size):
        start = index * rows_x if group == 0 else lax.rem(index, half) * rows_x
        return pl.ds(start + i, size)

    def place(group, source, c, size):
        start = source * full if group == 0 else low + line.place(line.side, source) * shared
        return pl.ds(start + c, size)

    def a_near(c, s, source):
        _, index = line.near(s)
        return remote(full_a.at[pl.ds(index * rows_x, rows_x), pl.ds(c * PIECE, PIECE)],
                      early.at[:, pl.ds(source * full + c * PIECE, PIECE)],
                      a_send.at[c, s], a_recv.at[c, s], "gx", index)

    def a_self(c):
        return pltpu.make_async_copy(
            full_a.at[pl.ds(me * rows_x, rows_x), pl.ds(c * PIECE, PIECE)],
            early.at[:, pl.ds(me * full + c * PIECE, PIECE)], a_own.at[c])

    def s_near(i, s, source):
        pos, index = line.near(s)
        return remote(shared_a.at[rows_for(1, index, pos, i * STEP, STEP)],
                      early.at[pl.ds(i * STEP, STEP), place(1, source, 0, shared)],
                      s_send.at[i, s], s_recv.at[i, s], "gx", index)

    def s_self(i):
        return pltpu.make_async_copy(
            shared_a.at[rows_for(1, me, line.pos, i * STEP, STEP)],
            early.at[pl.ds(i * STEP, STEP), place(1, me, 0, shared)], s_own.at[i])

    def a_far_columns(c, p, source, slot):
        index = line.index(1 - line.side, p)
        return remote(full_a.at[pl.ds(index * rows_x, rows_x), pl.ds(c * PIECE, PIECE)],
                      early.at[:, pl.ds(source * full + c * PIECE, PIECE)],
                      ac_send.at[c, p], ac_recv.at[c, slot], "gx", index)

    def a_far_rows(i, p, source, slot):
        index = line.index(1 - line.side, p)
        return remote(full_a.at[pl.ds(index * rows_x + i * STEP, STEP)],
                      early.at[pl.ds(i * STEP, STEP), pl.ds(source * full, full)],
                      ax_send.at[i, p], ax_recv.at[i, slot], "gx", index)

    def b_near(i, group, s, source):
        pos, index = line.near(s)
        store = full_b if group == 0 else shared_b
        return remote(store.at[rows_for(group, index, pos, i * STEP, STEP)],
                      late.at[pl.ds(i * STEP, STEP), place(group, source, 0, full if group == 0 else shared)],
                      b_send.at[i, group, s], b_recv.at[i, group, s], "gx", index)

    def b_self(i, group):
        store = full_b if group == 0 else shared_b
        return pltpu.make_async_copy(
            store.at[rows_for(group, me, line.pos, i * STEP, STEP)],
            late.at[pl.ds(i * STEP, STEP), place(group, me, 0, full if group == 0 else shared)], b_own.at[i, group])

    def b_far(i, s, source):
        _, index = line.far(s)
        return remote(full_b.at[pl.ds(index * rows_x + i * STEP, STEP)],
                      late.at[pl.ds(i * STEP, STEP), pl.ds(source * full, full)],
                      bf_send.at[i, s], bf_recv.at[i, s], "gx", index)

    def z_part(n, s, source):
        slot, r, i = lax.rem(n, slots), n // steps, lax.rem(n, steps)
        target = lax.rem(my + s, count_gy)
        return remote(planes.at[slot, :, pl.ds(target * rows_y, rows_y)],
                      result.at[r, source, pl.ds(i * STEP, STEP)],
                      z_send.at[n, s], z_recv.at[n, s], "gy", target)

    def z_own(n):
        slot, r, i = lax.rem(n, slots), n // steps, lax.rem(n, steps)
        return pltpu.make_async_copy(
            planes.at[slot, :, pl.ds(my * rows_y, rows_y)],
            result.at[r, my, pl.ds(i * STEP, STEP)], z_send.at[n, 0])

    load(0, 0, 0).start()
    greet(count_gx, count_gy, me, my)

    kx = lax.broadcasted_iota(jnp.int32, (mid, lanes), 0)
    top = lax.broadcasted_iota(jnp.int32, (8, lanes), 0) == 0
    kx_sq = (kx * kx).astype(jnp.float32)
    lane = lax.broadcasted_iota(jnp.int32, (1, lanes), 1)
    kz = my * (lanes // 2) + jnp.where(lane < lanes // 2, lane, lane - lanes // 2)
    kz = jnp.where((kz == 0) & (lane >= lanes // 2), mid, kz)
    kz_sq = (kz * kz).astype(jnp.float32)

    def along_x(r, group, c, slot):
        source = loaded.at[slot].reshape(length * PIECE, lanes)
        cols = full if group == 0 else shared
        outs = length if group == 0 else length // 2
        store = ((full_a, shared_a), (full_b, shared_b))[r][group].reshape(outs * cols, lanes)
        scale = scales[r]

        def weigh(k, ky_sq):
            cosine = window(kx_sq + (ky_sq + kz_sq), scale)
            edge = window(float(mid) ** 2 + ky_sq + jnp.broadcast_to(kz_sq, (8, lanes)), scale)
            weights[k, :mid] = cosine
            weights[k, mid:] = cosine
            weights[k, mid:mid + 8] = jnp.where(top, edge, cosine[:8])

        def pair(j):
            freq = c * (PIECE // 2) + j
            if group == 0:
                freq = me * (full // 2) + freq
            else:
                freq = low // 2 + line.pos * (shared // 2) + freq
            weigh(0, (freq * freq).astype(jnp.float32))

            @pl.when(freq == 0)
            def _():
                weigh(1, float(mid) ** 2)
            other = 1 - (freq + mid - 1) // mid
            columns = [source[pl.ds(2 * j + k, length, stride=PIECE), :] for k in range(2)]
            spectrum = product(fwd_x[...], columns)
            weighted = [spectrum[0] * weights[0], spectrum[1] * weights[other]]
            matrix = inv_x[...] if group == 0 else inv_x[pl.ds(line.side * outs, outs)]
            out = product(matrix, weighted)
            for k in range(2):
                store[pl.ds(c * PIECE + 2 * j + k, outs, stride=cols), :] = out[k]

        loop(0, PIECE // 2, pair)

    inner_places, outer_places = range(half // 2), range(half // 2, half)
    outer = jnp.logical_not(line.inner)

    def x_pass(r, sent):
        def full_piece(c):
            @pl.when(c + 1 < count_f)
            def _():
                load(0, c + 1, lax.rem(c + 1, 2)).start()

            @pl.when(c + 1 == count_f)
            def _():
                load(1, 0, count_f % 2).start()
            load(0, c, lax.rem(c, 2)).wait()
            along_x(r, 0, c, lax.rem(c, 2))
            if r == 0:
                @pl.when(line.inner)
                def _():
                    for p in inner_places:
                        a_far_columns(c, p, me, line.pos).start()
                for s in range(1, half):
                    a_near(c, s, me).start()
                a_self(c).start()

        loop(0, count_f, full_piece)
        sent()

        def shared_piece(c):
            @pl.when(c + 1 < count_s)
            def _():
                load(1, c + 1, lax.rem(count_f + c + 1, 2)).start()
            load(1, c, lax.rem(count_f + c, 2)).wait()
            along_x(r, 1, c, lax.rem(count_f + c, 2))

        loop(0, count_s, shared_piece)

    def inner_rows():
        @pl.when(line.inner)
        def _():
            def send(i):
                for p in outer_places:
                    a_far_rows(i, p, me, line.pos).start()
            loop(0, steps, send)

    x_pass(0, inner_rows)

    def send_rows(i):
        for s in range(1, half):
            s_near(i, s, me).start()
        s_self(i).start()

        @pl.when(outer)
        def _():
            for p in range(half):
                a_far_rows(i, p, me, line.pos).start()

    loop(0, steps, send_rows)
    load(0, 0, 0).start()
    x_pass(1, lambda: None)

    def along_y(n, bring):
        bring.start()

        @pl.when(n >= slots)
        def _():
            for s in range(1, count_gy):
                z_part(n - slots, s, my).wait_send()
            z_own(n - slots).wait()
        bring.wait()
        slot = lax.rem(n, slots)

        def pair(j):
            out = product(inv_y[...], [lines[2 * j], lines[2 * j + 1]])
            planes[slot, 2 * j] = out[0]
            planes[slot, 2 * j + 1] = out[1]

        loop(0, STEP // 2, pair)
        for s in range(1, count_gy):
            z_part(n, s, my).start()
        z_own(n).start()

    def near_source(s):
        return line.index(line.side, lax.rem(line.pos + half - s, half))

    def far_source(pos):
        return line.index(1 - line.side, pos)

    def send_b_near(i):
        for group in range(2):
            for s in range(1, half):
                b_near(i, group, s, me).start()
            b_self(i, group).start()

    def send_b_far(i):
        for s in range(half):
            b_far(i, s, me).start()

    batch = max(1, steps // 4)

    @pl.when(outer)
    def _():
        def send(n):
            loop(n * batch, (n + 1) * batch, send_b_near)
            loop(n * batch, (n + 1) * batch, send_b_far)
        loop(0, steps // batch, send)

    @pl.when(line.inner)
    def _():
        loop(0, steps, send_b_near)

    def wait_pieces(c):
        for s in range(1, half):
            a_near(c, s, near_source(s)).wait_recv()
        a_self(c).wait()

        @pl.when(line.inner)
        def _():
            for p in inner_places:
                a_far_columns(c, p, far_source(p), p).wait_recv()

    loop(0, count_f, wait_pieces)

    def first_rows(i):
        for s in range(1, half):
            s_near(i, s, near_source(s)).wait_recv()
        s_self(i).wait()
        for p in outer_places:
            a_far_rows(i, p, far_source(p), p).wait_recv()

        @pl.when(outer)
        def _():
            for p in inner_places:
                a_far_rows(i, p, far_source(p), p).wait_recv()

        @pl.when(jnp.logical_and(line.inner, i == steps - 1))
        def _():
            loop(0, batch, send_b_far)
        along_y(i, pltpu.make_async_copy(early.at[pl.ds(i * STEP, STEP)], lines, line_sem))

    loop(0, steps, first_rows)

    def later_rows(i):
        for group in range(2):
            for s in range(1, half):
                b_near(i, group, s, near_source(s)).wait_recv()
            b_self(i, group).wait()
        for s in range(half):
            b_far(i, s, far_source(lax.rem(line.pos + half - s, half))).wait_recv()

        @pl.when(jnp.logical_and(line.inner, jnp.logical_and(lax.rem(i + 1, batch) == 0, i + 1 < steps)))
        def _():
            loop(i + 1, i + 1 + batch, send_b_far)
        along_y(steps + i, pltpu.make_async_copy(late.at[pl.ds(i * STEP, STEP)], lines, line_sem))

    loop(0, steps, later_rows)

    def drain_a(c):
        for s in range(1, half):
            a_near(c, s, me).wait_send()

        @pl.when(line.inner)
        def _():
            for p in inner_places:
                a_far_columns(c, p, me, line.pos).wait_send()

    loop(0, count_f, drain_a)

    def drain_b(i):
        for s in range(1, half):
            s_near(i, s, me).wait_send()
        for p in outer_places:
            a_far_rows(i, p, me, line.pos).wait_send()

        @pl.when(outer)
        def _():
            for p in inner_places:
                a_far_rows(i, p, me, line.pos).wait_send()
        for group in range(2):
            for s in range(1, half):
                b_near(i, group, s, me).wait_send()
        for s in range(half):
            b_far(i, s, me).wait_send()

    loop(0, steps, drain_b)

    def drain_sends(n):
        for s in range(1, count_gy):
            z_part(n, s, my).wait_send()
        z_own(n).wait()

    loop(max(0, 2 * steps - slots), 2 * steps, drain_sends)

    def drain_z(n):
        for s in range(1, count_gy):
            z_part(n, s, lax.rem(my + count_gy - s, count_gy)).wait_recv()

    loop(0, 2 * steps, drain_z)


def per_device(density, radius_cells):
    rows_x, rows_y, length = density.shape
    count_gx = lax.axis_size("gx")
    count_gy = lax.axis_size("gy")
    half = count_gx // 2
    lanes = length // count_gy
    full, shared = group_columns(length, count_gx)
    count_f, count_s = full // PIECE, shared // PIECE
    steps = rows_x // STEP
    assert full % PIECE == 0 and shared % PIECE == 0
    f32 = jnp.float32
    vmem = pl.BlockSpec(memory_space=pltpu.VMEM)
    hbm = pl.BlockSpec(memory_space=pl.ANY)
    dma = pltpu.SemaphoreType.DMA

    table_z, gain_z = basis(length, blocked(length, count_gy))
    table_y, gain_y = basis(length, paired(length))
    table_x, gain_x = basis(length, blocked(length, 1))
    flops = 2 * 3 * rows_x * rows_y * length * length

    cube = pl.pallas_call(
        functools.partial(forward_kernel, count_gx, count_gy),
        out_shape=jax.ShapeDtypeStruct((length, full + shared, lanes), f32),
        in_specs=[hbm, vmem, vmem],
        out_specs=hbm,
        scratch_shapes=[
            pltpu.VMEM((2, STEP, rows_y, length), f32),
            pltpu.VMEM((steps, count_gy, STEP, rows_y, lanes), f32),
            pltpu.VMEM((rows_x, length, lanes), f32),
            pltpu.VMEM((rows_x, length, lanes), f32),
            dma((2,)), dma((steps, count_gy)), dma((steps, count_gy)),
            dma((steps, 2, half)), dma((steps, 2, half)),
            dma((steps, 2, half)), dma((steps, 2, half)), dma((steps, 2)),
        ],
        compiler_params=pltpu.CompilerParams(
            collective_id=0, has_side_effects=True, vmem_limit_bytes=VMEM),
        cost_estimate=pl.CostEstimate(flops=2 * flops, bytes_accessed=8 * density.size, transcendentals=0),
        name="forward",
    )(density, tripled(table_z.T, 0), tripled(table_y, 1))

    scales = 2.0 * math.pi / length * radius_cells.astype(f32)
    slots = 4
    field = jax.ShapeDtypeStruct((rows_x, length, lanes), f32)
    _, _, fields = pl.pallas_call(
        functools.partial(inverse_kernel, count_gx, count_gy, rows_x, rows_y),
        out_shape=(field, field, jax.ShapeDtypeStruct((2, count_gy, rows_x, rows_y, lanes), f32)),
        in_specs=[pl.BlockSpec(memory_space=pltpu.SMEM), hbm, vmem, vmem, vmem],
        out_specs=(hbm, hbm, hbm),
        scratch_shapes=[
            pltpu.VMEM((2, length, PIECE, lanes), f32),
            pltpu.VMEM((2, length, lanes), f32),
            pltpu.VMEM((length, full, lanes), f32),
            pltpu.VMEM((length // 2, shared, lanes), f32),
            pltpu.VMEM((length, full, lanes), f32),
            pltpu.VMEM((length // 2, shared, lanes), f32),
            pltpu.VMEM((STEP, length, lanes), f32),
            pltpu.VMEM((slots, STEP, length, lanes), f32),
            dma((2,)),
            dma((count_f, half)), dma((count_f, half)), dma((count_f,)),
            dma((steps, half)), dma((steps, half)), dma((steps,)),
            dma((count_f, half)), dma((count_f, half)),
            dma((steps, half)), dma((steps, half)),
            dma((steps, 2, half)), dma((steps, 2, half)), dma((steps, 2)),
            dma((steps, half)), dma((steps, half)),
            dma(()), dma((2 * steps, count_gy)), dma((2 * steps, count_gy)),
        ],
        compiler_params=pltpu.CompilerParams(
            collective_id=1, has_side_effects=True, vmem_limit_bytes=VMEM),
        cost_estimate=pl.CostEstimate(flops=5 * flops, bytes_accessed=20 * density.size, transcendentals=0),
        name="inverse",
    )(scales * scales, cube, tripled(table_x, 1), tripled((table_x * gain_x).T, 1),
      tripled((table_y * gain_y).T, 1))

    inv_z = jnp.asarray(table_z * gain_z, f32).reshape(count_gy, lanes, length)
    return jnp.einsum("rgxyl,glz->rxyz", fields, inv_z,
                      precision=lax.Precision.HIGH, preferred_element_type=f32)


def solution(mesh):
    return jax.shard_map(
        per_device,
        mesh=mesh,
        in_specs=(P("gx", "gy", None), P()),
        out_specs=P(None, "gx", "gy", None),
        check_vma=False,
    )
```

time: 1340 us -> 1110 us (0.83)
  Pallas kernels: 1300 us -> 1070 us
    pallas_call x1, Pallas kernels: 907 us -> 541 us  [per_device(): pl.pallas_call(functools.partial(inverse_kernel, count_gx, count_gy, rows...]
    pallas_call x1, Pallas kernels: 397 us -> 531 us  [per_device(): pl.pallas_call(functools.partial(forward_kernel, count_gx, count_gy), out...]
where the time goes in v2:
time: 1110 us
  Pallas kernels  1070 us (96%)
  matrix products  33.2 us (3%)
    pallas_call x1, Pallas kernels, per_device(): pl.pallas_call(functools.partial(inverse_kernel, count_gx, count_gy, rows...  541 us
    pallas_call x1, Pallas kernels, per_device(): pl.pallas_call(functools.partial(forward_kernel, count_gx, count_gy), out...  531 us
    dot_general x1, matrix products, per_device(): jnp.einsum('rgxyl,glz->rxyz', fields, inv_z, precision=lax.Precision.HIGH...  33.2 us

profile of v2, /device:TPU:11, one launch (start us, length us, event | category | flops | bytes accessed | tf_op | source)
XLA Modules:
  0.0 1106.3 jit_solution(16627834524006519795)
XLA Ops:
  0.0 1.2 multiply_multiply_fusion.scales
  1.2 530.8 %forward.1.cube = f32[512,88,128]{2,1,0:T(8,128)} custom-call(f32[64,128,512]{2,1,0:T(8,128)} %density.1, bf16[1536,512]{1,0:T(8,128)(2,1)} %constant.24.fwd_z, bf16[512,1536]{1,0:T(8,128)(2,1)} %constant.29.fwd_y), custom_call_target="tpu_custom_call" | custom-call | flops 25769803776 | bytes 33554432 | tf_op jit(solution)/shard_map/forward/pallas_call | solution.py:603
  532.0 541.1 %inverse.1 = (f32[64,512,128]{2,1,0:T(8,128)}, f32[64,512,128]{2,1,0:T(8,128)}, f32[2,4,64,128,128]{4,3,2,1,0:T(8,128)}) custom-call(f32[2]{0:T(128)} %multiply_multiply_fusion.scales, f32[512,88,128]{2,1,0:T(8,128)} %forward.1.cube, bf16[512,1536]{1,0:T(8,128)(2,1)} %constant.34.fwd_x, bf16[512,1536]{1,0:T(8,128)(2,1)} %constant.39.inv_x, ...), custom_call_target="tpu_custom_call" | custom-call | flops 64424509440 | bytes 83886080 | tf_op jit(solution)/shard_map/inverse/pallas_call | solution.py:626
  1073.1 33.2 %convolution_bitcast_fusion = f32[2,64,128,512]{3,2,1,0:T(8,128)} fusion(f32[2,4,64,128,128]{4,3,2,1,0:T(8,128)} %get-tuple-element.6, f32[4,128,512,1,1]{2,1,0,4,3:T(8,128)} %constant.46), kind=kOutput, calls=%fused_computation | convolution fusion | flops 25769803776 | bytes 68157440 | tf_op jit(solution)/shard_map/rgxyl,glz->rxyz/dot_general | solution.py:657

commit v3 on v2

--- a/solution.py
+++ b/solution.py
@@ -10,7 +10,7 @@
 from jax.sharding import PartitionSpec as P
 
 MESH = pl.DeviceIdType.MESH
-STEP = 8
+STEP = 4
 PIECE = 8
 VMEM = 63 * 1024 * 1024
 
@@ -196,9 +196,13 @@
             z_part(i, s, my).start()
         z_own(i).start()
 
-    loop(0, steps, along_z)
+    lead = min(4, steps)
+    loop(0, lead, along_z)
 
     def along_y(i):
+        @pl.when(i + lead < steps)
+        def _():
+            along_z(i + lead)
         for s in range(1, count_gy):
             z_part(i, s, lax.rem(my + count_gy - s, count_gy)).wait_recv()
         z_own(i).wait()
@@ -244,11 +248,12 @@
 
 def inverse_kernel(count_gx, count_gy, rows_x, rows_y, scales, cube, fwd_x, inv_x, inv_y,
                    early, late, result, loaded, weights, full_a, shared_a, full_b, shared_b, lines, planes,
-                   load_sem, a_send, a_recv, a_own, s_send, s_recv, s_own, ac_send, ac_recv, ax_send, ax_recv,
+                   load_sem, a_send, a_recv, a_own, c_send, c_recv, c_own, s_send, s_recv, s_own, ac_send, ac_recv, ax_send, ax_recv,
                    b_send, b_recv, b_own, bf_send, bf_recv, line_sem, z_send, z_recv):
     length, _, lanes = cube.shape
     full, shared = group_columns(length, count_gx)
     count_f, count_s = full // PIECE, shared // PIECE
+    count_c = c_own.shape[0]
     steps = rows_x // STEP
     mid = length // 2
     line = Line(count_gx)
@@ -280,16 +285,29 @@
             full_a.at[pl.ds(me * rows_x, rows_x), pl.ds(c * PIECE, PIECE)],
             early.at[:, pl.ds(me * full + c * PIECE, PIECE)], a_own.at[c])
 
+    def c_near(c, s, source):
+        pos, index = line.near(s)
+        return remote(shared_a.at[rows_for(1, index, pos, 0, rows_x), pl.ds(c * PIECE, PIECE)],
+                      early.at[:, place(1, source, c * PIECE, PIECE)],
+                      c_send.at[c, s], c_recv.at[c, s], "gx", index)
+
+    def c_self(c):
+        return pltpu.make_async_copy(
+            shared_a.at[rows_for(1, me, line.pos, 0, rows_x), pl.ds(c * PIECE, PIECE)],
+            early.at[:, place(1, me, c * PIECE, PIECE)], c_own.at[c])
+
+    done = count_c * PIECE
+
     def s_near(i, s, source):
         pos, index = line.near(s)
-        return remote(shared_a.at[rows_for(1, index, pos, i * STEP, STEP)],
-                      early.at[pl.ds(i * STEP, STEP), place(1, source, 0, shared)],
+        return remote(shared_a.at[rows_for(1, index, pos, i * STEP, STEP), pl.ds(done, shared - done)],
+                      early.at[pl.ds(i * STEP, STEP), place(1, source, done, shared - done)],
                       s_send.at[i, s], s_recv.at[i, s], "gx", index)
 
     def s_self(i):
         return pltpu.make_async_copy(
-            shared_a.at[rows_for(1, me, line.pos, i * STEP, STEP)],
-            early.at[pl.ds(i * STEP, STEP), place(1, me, 0, shared)], s_own.at[i])
+            shared_a.at[rows_for(1, me, line.pos, i * STEP, STEP), pl.ds(done, shared - done)],
+            early.at[pl.ds(i * STEP, STEP), place(1, me, done, shared - done)], s_own.at[i])
 
     def a_far_columns(c, p, source, slot):
         index = line.index(1 - line.side, p)
@@ -385,7 +403,7 @@
     inner_places, outer_places = range(half // 2), range(half // 2, half)
     outer = jnp.logical_not(line.inner)
 
-    def x_pass(r, sent):
+    def x_pass(sent):
         def full_piece(c):
             @pl.when(c + 1 < count_f)
             def _():
@@ -395,15 +413,15 @@
             def _():
                 load(1, 0, count_f % 2).start()
             load(0, c, lax.rem(c, 2)).wait()
-            along_x(r, 0, c, lax.rem(c, 2))
-            if r == 0:
-                @pl.when(line.inner)
-                def _():
-                    for p in inner_places:
-                        a_far_columns(c, p, me, line.pos).start()
-                for s in range(1, half):
-                    a_near(c, s, me).start()
-                a_self(c).start()
+            along_x(0, 0, c, lax.rem(c, 2))
+
+            @pl.when(line.inner)
+            def _():
+                for p in inner_places:
+                    a_far_columns(c, p, me, line.pos).start()
+            for s in range(1, half):
+                a_near(c, s, me).start()
+            a_self(c).start()
 
         loop(0, count_f, full_piece)
         sent()
@@ -413,7 +431,13 @@
             def _():
                 load(1, c + 1, lax.rem(count_f + c + 1, 2)).start()
             load(1, c, lax.rem(count_f + c, 2)).wait()
-            along_x(r, 1, c, lax.rem(count_f + c, 2))
+            along_x(0, 1, c, lax.rem(count_f + c, 2))
+
+            @pl.when(c < count_c)
+            def _():
+                for s in range(1, half):
+                    c_near(c, s, me).start()
+                c_self(c).start()
 
         loop(0, count_s, shared_piece)
 
@@ -425,7 +449,7 @@
                     a_far_rows(i, p, me, line.pos).start()
             loop(0, steps, send)
 
-    x_pass(0, inner_rows)
+    x_pass(inner_rows)
 
     def send_rows(i):
         for s in range(1, half):
@@ -439,7 +463,6 @@
 
     loop(0, steps, send_rows)
     load(0, 0, 0).start()
-    x_pass(1, lambda: None)
 
     def along_y(n, bring):
         bring.start()
@@ -478,18 +501,46 @@
         for s in range(half):
             b_far(i, s, me).start()
 
-    batch = max(1, steps // 4)
-
-    @pl.when(outer)
-    def _():
-        def send(n):
-            loop(n * batch, (n + 1) * batch, send_b_near)
-            loop(n * batch, (n + 1) * batch, send_b_far)
-        loop(0, steps // batch, send)
-
-    @pl.when(line.inner)
-    def _():
-        loop(0, steps, send_b_near)
+    batch = max(1, steps // 8)
+
+    def send_second():
+        @pl.when(outer)
+        def _():
+            def send(n):
+                loop(n * batch, (n + 1) * batch, send_b_near)
+                loop(n * batch, (n + 1) * batch, send_b_far)
+            loop(0, steps // batch, send)
+
+        @pl.when(line.inner)
+        def _():
+            loop(0, steps, send_b_near)
+
+    count = count_f + count_s
+
+    def second_piece(n):
+        slot = lax.rem(n, 2)
+
+        @pl.when(n + 1 < count_f)
+        def _():
+            load(0, n + 1, 1 - slot).start()
+
+        @pl.when(jnp.logical_and(n + 1 >= count_f, n + 1 < count))
+        def _():
+            load(1, n + 1 - count_f, 1 - slot).start()
+
+        @pl.when(n < count_f)
+        def _():
+            load(0, n, slot).wait()
+            along_x(1, 0, n, slot)
+
+        @pl.when(n >= count_f)
+        def _():
+            load(1, n - count_f, slot).wait()
+            along_x(1, 1, n - count_f, slot)
+
+        @pl.when(n == count - 1)
+        def _():
+            send_second()
 
     def wait_pieces(c):
         for s in range(1, half):
@@ -501,9 +552,20 @@
             for p in inner_places:
                 a_far_columns(c, p, far_source(p), p).wait_recv()
 
-    loop(0, count_f, wait_pieces)
+    def wait_shared(c):
+        for s in range(1, half):
+            c_near(c, s, near_source(s)).wait_recv()
+        c_self(c).wait()
 
     def first_rows(i):
+        @pl.when(i < count)
+        def _():
+            second_piece(i)
+
+        @pl.when(i == 0)
+        def _():
+            loop(0, count_f, wait_pieces)
+            loop(0, count_c, wait_shared)
         for s in range(1, half):
             s_near(i, s, near_source(s)).wait_recv()
         s_self(i).wait()
@@ -547,6 +609,12 @@
                 a_far_columns(c, p, me, line.pos).wait_send()
 
     loop(0, count_f, drain_a)
+
+    def drain_c(c):
+        for s in range(1, half):
+            c_near(c, s, me).wait_send()
+
+    loop(0, count_c, drain_c)
 
     def drain_b(i):
         for s in range(1, half):
@@ -589,7 +657,8 @@
     full, shared = group_columns(length, count_gx)
     count_f, count_s = full // PIECE, shared // PIECE
     steps = rows_x // STEP
-    assert full % PIECE == 0 and shared % PIECE == 0
+    count_c = max(1, count_s // 3)
+    assert full % PIECE == 0 and shared % PIECE == 0 and count_f + count_s <= steps
     f32 = jnp.float32
     vmem = pl.BlockSpec(memory_space=pltpu.VMEM)
     hbm = pl.BlockSpec(memory_space=pl.ANY)
@@ -621,7 +690,7 @@
     )(density, tripled(table_z.T, 0), tripled(table_y, 1))
 
     scales = 2.0 * math.pi / length * radius_cells.astype(f32)
-    slots = 4
+    slots = 8
     field = jax.ShapeDtypeStruct((rows_x, length, lanes), f32)
     _, _, fields = pl.pallas_call(
         functools.partial(inverse_kernel, count_gx, count_gy, rows_x, rows_y),
@@ -639,6 +708,7 @@
             pltpu.VMEM((slots, STEP, length, lanes), f32),
             dma((2,)),
             dma((count_f, half)), dma((count_f, half)), dma((count_f,)),
+            dma((count_c, half)), dma((count_c, half)), dma((count_c,)),
             dma((steps, half)), dma((steps, half)), dma((steps,)),
             dma((count_f, half)), dma((count_f, half)),
             dma((steps, half)), dma((steps, half)),

time: 1110 us -> 1100 us (level); the launches traced: 1110 us -> 1080 us
  Pallas kernels: 1070 us -> 1050 us
    pallas_call x1, Pallas kernels: 541 us -> 527 us  [per_device(): pl.pallas_call(functools.partial(inverse_kernel, count_gx, count_gy, rows...]
where the time goes in v3:
time: 1100 us; the launch traced here: 1080 us
  Pallas kernels  1050 us (95%)
  matrix products  33.2 us (3%)
    pallas_call x1, Pallas kernels, per_device(): pl.pallas_call(functools.partial(inverse_kernel, count_gx, count_gy, rows...  527 us
    pallas_call x1, Pallas kernels, per_device(): pl.pallas_call(functools.partial(forward_kernel, count_gx, count_gy), out...  522 us
    dot_general x1, matrix products, per_device(): jnp.einsum('rgxyl,glz->rxyz', fields, inv_z, precision=lax.Precision.HIGH...  33.2 us

profile of v3, /device:TPU:11, one launch (start us, length us, event | category | flops | bytes accessed | tf_op | source)
XLA Modules:
  0.0 1083.4 jit_solution(4556894841885329485)
XLA Ops:
  0.0 1.2 multiply_multiply_fusion.scales
  1.2 521.6 %forward.1.cube = f32[512,88,128]{2,1,0:T(8,128)} custom-call(f32[64,128,512]{2,1,0:T(8,128)} %density.1, bf16[1536,512]{1,0:T(8,128)(2,1)} %constant.24.fwd_z, bf16[512,1536]{1,0:T(8,128)(2,1)} %constant.29.fwd_y), custom_call_target="tpu_custom_call" | custom-call | flops 25769803776 | bytes 33554432 | tf_op jit(solution)/shard_map/forward/pallas_call | solution.py:672
  522.7 527.5 %inverse.1 = (f32[64,512,128]{2,1,0:T(8,128)}, f32[64,512,128]{2,1,0:T(8,128)}, f32[2,4,64,128,128]{4,3,2,1,0:T(8,128)}) custom-call(f32[2]{0:T(128)} %multiply_multiply_fusion.scales, f32[512,88,128]{2,1,0:T(8,128)} %forward.1.cube, bf16[512,1536]{1,0:T(8,128)(2,1)} %constant.34.fwd_x, bf16[512,1536]{1,0:T(8,128)(2,1)} %constant.39.inv_x, ...), custom_call_target="tpu_custom_call" | custom-call | flops 64424509440 | bytes 83886080 | tf_op jit(solution)/shard_map/inverse/pallas_call | solution.py:695
  1050.2 33.2 %convolution_bitcast_fusion = f32[2,64,128,512]{3,2,1,0:T(8,128)} fusion(f32[2,4,64,128,128]{4,3,2,1,0:T(8,128)} %get-tuple-element.6, f32[4,128,512,1,1]{2,1,0,4,3:T(8,128)} %constant.46), kind=kOutput, calls=%fused_computation | convolution fusion | flops 25769803776 | bytes 68157440 | tf_op jit(solution)/shard_map/rgxyl,glz->rxyz/dot_general | solution.py:727
